TPU v7x, 512 devices: a whole 4x8x8 slice. The times are simulated.
512 devices in a mesh: wide: 128 (over z, y, core), quad: 4 (over x).
Axes of the slice: x: 4, y: 8, z: 8, core: 2. Of those that a mesh axis runs over, the one named last changes fastest.
Arguments:
- orbitals: float32 [256, 64, 4096], P('wide', 'quad'), may hold values from -6 to 6
- corners: int32 [256, 2], P('wide'), may hold values from 0 to 16
- pair_partner: int32 [512], P('wide'), may hold values from 0 to 255, as said below
- pair_live: int32 [512], P('wide'), may hold values from 0 to 1, as said below
Outputs:
- exchange_action: float32 [256, 64, 4096], P('wide', 'quad')
Inputs may be any that keep to these rules, and one draw needn't show every extreme that they name: For the slots of owner w, the second orbital lies between the first plus 1 and the first plus 4 where the slot is live; every pair_partner is a valid orbital index. The number of live slots differs from owner to owner, and owner 0 has all 4 live. `pair_live`: dead slots may stand anywhere among an owner's slots.
All inputs are finite; a program needn't handle non-finite values.
Results may differ from a plain program's by a relative error of at most 0.0003.
Values sent between devices are 32-bit elements; how exact they have to be, the bound alone decides.
No kernel may reach another device: no remote copies, remote signals or barrier semaphores. Data moves between devices by JAX's collectives and lax.ppermute only.
A program may use at most 64 MiB of HBM per device.

v0:
```python
import math

import jax
import jax.numpy as jnp
from jax import lax
from jax.sharding import PartitionSpec as P

BZ = 64
SPAN = 16
SWEEPS = 8


def passed_along(x, axis, by):
    size = lax.axis_size(axis)
    pairs = [(i, i + by) for i in range(size) if 0 <= i + by < size]
    return lax.ppermute(x, axis, pairs)


def in_blocks(x, dim, size):
    lengths = x.shape
    pieces = x.reshape(*lengths[:dim], size, lengths[dim] // size, *lengths[dim + 1 :])
    return jnp.moveaxis(pieces, dim, 0)


def edges_of(length, count):
    hop = length // count
    if hop >= 8:
        hop -= hop % 8
    return [hop * k for k in range(1, count)]


def joined_along(pieces, dim):
    pieces = jnp.moveaxis(pieces, 0, dim)
    lengths = pieces.shape
    return pieces.reshape(*lengths[:dim], lengths[dim] * lengths[dim + 1], *lengths[dim + 2 :])


def exchange_in_pieces(x, axis, pieces, split_dim, concat_dim):
    blocks = in_blocks(x, split_dim, lax.axis_size(axis))
    cut = max(range(1, max(2, blocks.ndim - 1)), key=lambda d: blocks.shape[d])
    outs = []
    for slab in jnp.split(blocks, edges_of(blocks.shape[cut], pieces), axis=cut):
        if slab.size:
            outs.append(lax.all_to_all(slab, axis, split_axis=0, concat_axis=0, tiled=True))
    return joined_along(jnp.concatenate(outs, axis=cut), concat_dim)


def sweep_weights():
    low = 0.5 / 6.5
    high = 12.5 / 6.5
    center = (high + low) / 2.0
    half = (high - low) / 2.0
    return [
        1.0 / (center + half * math.cos(math.pi * (2 * k + 1) / (2 * SWEEPS)))
        for k in range(SWEEPS)
    ]


def move_box(box, shift_y, shift_z):
    margin = SPAN * BZ + SPAN
    flat = box.shape[-1]
    padded = jnp.pad(box, ((0, 0), (margin, margin)))
    start = margin - shift_y * BZ - shift_z
    taken = lax.dynamic_slice_in_dim(padded, start, flat, 1)
    source = jnp.arange(flat, dtype=jnp.int32) % BZ - shift_z
    keep = (source >= 0) & (source < BZ)
    return jnp.where(keep[None, :], taken, jnp.zeros_like(taken))


def neighbours(field, padded):
    flat = field.shape[-1]
    zpos = jnp.arange(flat, dtype=jnp.int32) % BZ
    total = padded[:, 2:] + padded[:, :-2]
    upper_z = jnp.pad(field[..., 1:], ((0, 0), (0, 0), (0, 1)))
    lower_z = jnp.pad(field[..., :-1], ((0, 0), (0, 0), (1, 0)))
    total = total + jnp.where(zpos < BZ - 1, upper_z, 0.0) + jnp.where(zpos > 0, lower_z, 0.0)
    total = total + jnp.pad(field[..., BZ:], ((0, 0), (0, 0), (0, BZ)))
    total = total + jnp.pad(field[..., :-BZ], ((0, 0), (0, 0), (BZ, 0)))
    return total


def solve_boxes(density):
    weights = sweep_weights()
    potential = weights[0] * density / 6.5
    for k in range(1, SWEEPS):
        padded = jnp.pad(potential, ((0, 0), (1, 1), (0, 0)))
        applied = 6.5 * potential - neighbours(potential, padded)
        potential = potential + weights[k] * (density - applied) / 6.5
    return potential


def per_device(orbitals, corners, pair_partner, pair_live):
    per_owner = orbitals.shape[0]
    slot_count = pair_partner.shape[0]
    base = lax.axis_index("wide") * per_owner
    corner_float = corners.astype(jnp.float32)
    pool_orbs = [orbitals]
    pool_corners = [corner_float]
    for step in range(1, 3):
        ahead, ahead_corners = passed_along((orbitals, corner_float), "wide", -step)
        pool_orbs.append(ahead)
        pool_corners.append(ahead_corners)
    pool = jnp.concatenate(pool_orbs, axis=0)
    pool_corner = jnp.concatenate(pool_corners, axis=0).astype(jnp.int32)
    width = pool.shape[0]
    left_index = jnp.arange(slot_count, dtype=jnp.int32) % per_owner
    right_index = jnp.clip(pair_partner - base, 0, width - 1)
    own = orbitals[left_index]
    offset = pool_corner[right_index] - corners[left_index]
    moved = jax.vmap(move_box)(pool[right_index], offset[:, 0], offset[:, 1])
    density = own * moved * pair_live.astype(jnp.float32)[:, None, None]
    boxes = lax.all_to_all(density, "quad", split_axis=0, concat_axis=1, tiled=True)
    potential = exchange_in_pieces(solve_boxes(boxes), "quad", 2, 1, 0)
    left_terms = potential * moved
    right_terms = jax.vmap(move_box)(potential * own, -offset[:, 0], -offset[:, 1])
    rows = jnp.arange(width, dtype=jnp.int32)[:, None]
    left_table = (rows == left_index[None, :]).astype(jnp.float32)
    right_table = (rows == right_index[None, :]).astype(jnp.float32)
    gathered = jnp.einsum("op,pxf->oxf", left_table, left_terms, precision=lax.Precision.HIGHEST)
    gathered = gathered + jnp.einsum(
        "op,pxf->oxf", right_table, right_terms, precision=lax.Precision.HIGHEST
    )
    result = gathered[:per_owner]
    for step in range(1, 3):
        segment = gathered[step * per_owner : (step + 1) * per_owner]
        result = result + passed_along(segment, "wide", step)
    return result


def solution(mesh):
    in_specs = (P("wide", "quad", None), P("wide", None), P("wide"), P("wide"))
    out_specs = P("wide", "quad", None)
    return jax.shard_map(
        per_device, mesh=mesh, in_specs=in_specs, out_specs=out_specs, check_vma=False
    )
```

profile of v0, /device:TPU:257, one launch (start us, length us, event | category | flops | bytes accessed | tf_op | source)
XLA Modules:
  0.0 146.4 jit_solution(1997866902169364131)
XLA Ops:
  0.0 0.8 copy.11
  0.8 2.6 %collective-permute-start = (f32[2,2]{0,1:T(2,128)S(1)}, f32[2,2]{0,1:T(2,128)S(1)}, u32[]{:S(2)}, u32[]{:S(2)}) collective-permute-start(f32[2,2]{0,1:T(2,128)S(1)} %convert_element_type.54), channel_id=1, source_target_pairs={{4,0},{8,4},{12,8},{16,12},{20,16},{24,20},{28,24},{32,28},{36,32}... | collective-permute-start | bytes 56 | tf_op jit(solution)/shard_map/ppermute | solution.py:16
  3.4 4.2 %collective-permute-start.1 = (f32[2,2]{0,1:T(2,128)S(1)}, f32[2,2]{0,1:T(2,128)S(1)}, u32[]{:S(2)}, u32[]{:S(2)}) collective-permute-start(f32[2,2]{0,1:T(2,128)S(1)} %convert_element_type.54), channel_id=1, source_target_pairs={{8,0},{12,4},{16,8},{20,12},{24,16},{28,20},{32,24},{36,28},{40,32... | collective-permute-start | bytes 56 | tf_op jit(solution)/shard_map/ppermute | solution.py:16
  7.6 3.0 %collective-permute-start.2 = (f32[2,16,4096]{2,1,0:T(8,128)}, f32[2,16,4096]{2,1,0:T(8,128)S(1)}, u32[]{:S(2)}, u32[]{:S(2)}) collective-permute-start(f32[2,16,4096]{2,1,0:T(8,128)} %param.4), channel_id=1, source_target_pairs={{4,0},{8,4},{12,8},{16,12},{20,16},{24,20},{28,24},{32,28},{36,32}... | collective-permute-start | bytes 1572872 | tf_op jit(solution)/shard_map/ppermute | solution.py:16
  10.6 3.0 %collective-permute-start.3 = (f32[2,16,4096]{2,1,0:T(8,128)}, f32[2,16,4096]{2,1,0:T(8,128)}, u32[]{:S(2)}, u32[]{:S(2)}) collective-permute-start(f32[2,16,4096]{2,1,0:T(8,128)} %param.4), channel_id=1, source_target_pairs={{8,0},{12,4},{16,8},{20,12},{24,16},{28,20},{32,24},{36,28},{40,32... | collective-permute-start | bytes 1572872 | tf_op jit(solution)/shard_map/ppermute | solution.py:16
  13.7 1.2 gather_fusion.2
  15.0 1.7 %gather_fusion = f32[4,16,4096]{2,1,0:T(8,128)S(1)} fusion(f32[2,16,4096]{2,1,0:T(8,128)} %param.4, s32[1024]{0:T(1024)S(1)} %pad_clamp_fusion.1), kind=kCustom, calls=%fused_computation | custom fusion | bytes 2097168 | tf_op jit(solution)/shard_map/gather | solution.py:108
  16.9 0.6 gather_fusion.1
  17.9 3.6 %collective-permute-done.2 = f32[2,16,4096]{2,1,0:T(8,128)S(1)} collective-permute-done((f32[2,16,4096]{2,1,0:T(8,128)}, f32[2,16,4096]{2,1,0:T(8,128)S(1)}, u32[]{:S(2)}, u32[]{:S(2)}) %collective-permute-start.2) | collective-permute-done | bytes 524320 | tf_op jit(solution)/shard_map/ppermute | solution.py:16
  21.5 0.8 copy-done.1
  22.3 4.4 %collective-permute-done.3 = f32[2,16,4096]{2,1,0:T(8,128)} collective-permute-done((f32[2,16,4096]{2,1,0:T(8,128)}, f32[2,16,4096]{2,1,0:T(8,128)}, u32[]{:S(2)}, u32[]{:S(2)}) %collective-permute-start.3) | collective-permute-done | bytes 524320 | tf_op jit(solution)/shard_map/ppermute | solution.py:16
  26.8 1.3 pad_maximum_fusion
  28.1 1.6 %gather_fusion.3 = f32[4,16,4096]{2,1,0:T(8,128)} fusion(f32[6,16,4096]{2,1,0:T(8,128)S(1)} %pad_maximum_fusion, s32[1024]{0:T(1024)S(1)} %pad_clamp_fusion), kind=kCustom, calls=%fused_computation.3 | custom fusion | bytes 2097168 | tf_op jit(solution)/shard_map/gather | solution.py:110
  29.7 2.8 %pad.119 = f32[4,16,6176]{2,1,0:T(8,128)} pad(f32[4,16,4096]{2,1,0:T(8,128)} %gather_fusion.3, f32[]{:T(128)} %constant.114.clone.1), padding=0_0x0_0x1040_1040 | pad | bytes 2629636 | tf_op jit(solution)/shard_map/vmap(jit(_pad))/pad | solution.py:62
  32.5 11.9 %while.2 = (s32[]{:T(128)}, f32[4,16,6176]{2,1,0:T(8,128)}, s32[4,3]{1,0:T(4,128)S(1)}, f32[4,16,4096]{2,1,0:T(8,128)S(1)}, s32[]{:T(128)}) while((s32[]{:T(128)}, f32[4,16,6176]{2,1,0:T(8,128)}, s32[4,3]{1,0:T(4,128)S(1)}, f32[4,16,4096]{2,1,0:T(8,128)S(1)}, s32[]{:T(128)}) %tuple.58), condition=%wide.while_cond, body=%wide.while_body.sunk | while | flops 2 | bytes 524405 | solution.py:64
  32.5 0.6 fusion.103
  33.1 2.3 %dynamic-slice_dynamic-update-slice_fusion.4 = f32[4,16,4096]{2,1,0:T(8,128)S(1)} fusion(f32[4,16,4096]{2,1,0:T(8,128)S(1)} %get-tuple-element.155, s32[]{:T(128)} %get-tuple-element.152, f32[4,16,6176]{2,1,0:T(8,128)} %get-tuple-element.158, s32[]{:T(128)} %bitcast.41, s32[]{:T(128)} %bitcast.42), kind=kLoop, calls=%fused_computation.4.clone.1 | loop fusion | bytes 524300 | tf_op jit(solution)/shard_map/vmap()/gather
  35.5 0.6 fusion.103
  36.1 2.3 %dynamic-slice_dynamic-update-slice_fusion.4 = f32[4,16,4096]{2,1,0:T(8,128)S(1)} fusion(f32[4,16,4096]{2,1,0:T(8,128)S(1)} %get-tuple-element.155, s32[]{:T(128)} %get-tuple-element.152, f32[4,16,6176]{2,1,0:T(8,128)} %get-tuple-element.158, s32[]{:T(128)} %bitcast.41, s32[]{:T(128)} %bitcast.42), kind=kLoop, calls=%fused_computation.4.clone.1 | loop fusion | bytes 524300 | tf_op jit(solution)/shard_map/vmap()/gather
  38.5 0.6 fusion.103
  39.1 2.3 %dynamic-slice_dynamic-update-slice_fusion.4 = f32[4,16,4096]{2,1,0:T(8,128)S(1)} fusion(f32[4,16,4096]{2,1,0:T(8,128)S(1)} %get-tuple-element.155, s32[]{:T(128)} %get-tuple-element.152, f32[4,16,6176]{2,1,0:T(8,128)} %get-tuple-element.158, s32[]{:T(128)} %bitcast.41, s32[]{:T(128)} %bitcast.42), kind=kLoop, calls=%fused_computation.4.clone.1 | loop fusion | bytes 524300 | tf_op jit(solution)/shard_map/vmap()/gather
  41.4 0.6 fusion.103
  42.0 2.3 %dynamic-slice_dynamic-update-slice_fusion.4 = f32[4,16,4096]{2,1,0:T(8,128)S(1)} fusion(f32[4,16,4096]{2,1,0:T(8,128)S(1)} %get-tuple-element.155, s32[]{:T(128)} %get-tuple-element.152, f32[4,16,6176]{2,1,0:T(8,128)} %get-tuple-element.158, s32[]{:T(128)} %bitcast.41, s32[]{:T(128)} %bitcast.42), kind=kLoop, calls=%fused_computation.4.clone.1 | loop fusion | bytes 524300 | tf_op jit(solution)/shard_map/vmap()/gather
  44.4 1.2 multiply_multiply_fusion
  45.6 4.0 %all-to-all-start = ((f32[4,16,4096]{2,1,0:T(8,128)}), f32[4,16,4096]{2,1,0:T(8,128)S(1)}, u32[]{:S(2)}, u32[]{:S(2)}) async-start(f32[4,16,4096]{2,1,0:T(8,128)} %multiply_multiply_fusion), calls=%async_computation | async-start | bytes 2097152 | tf_op jit(solution)/shard_map/all_to_all | solution.py:112
  49.6 11.0 %all-to-all-done = f32[4,16,4096]{2,1,0:T(8,128)S(1)} async-done(((f32[4,16,4096]{2,1,0:T(8,128)}), f32[4,16,4096]{2,1,0:T(8,128)S(1)}, u32[]{:S(2)}, u32[]{:S(2)}) %all-to-all-start) | async-done | bytes 1048608 | tf_op jit(solution)/shard_map/all_to_all | solution.py:112
  61.1 0.4 fusion.100
  61.4 0.9 fusion.8
  62.6 0.4 fusion.98
  63.0 0.8 fusion.17
  64.2 0.4 fusion.96
  64.5 0.8 fusion.26
  65.7 0.4 fusion.94
  66.1 0.8 fusion.35
  67.3 0.4 fusion.92
  67.7 0.8 fusion.44
  68.9 0.4 fusion.90
  69.2 0.8 fusion.53
  70.8 0.8 fusion.62
  71.6 0.9 fusion.86
  72.5 10.0 %all_to_all.22 = f32[4,1,8,4096]{3,2,1,0:T(8,128)} all-to-all(f32[4,1,8,4096]{3,2,1,0:T(8,128)S(1)} %get-tuple-element.49), channel_id=1, replica_groups=mesh['wide'=128,'quad'=4] {'quad'}, dimensions={0} | all-to-all | bytes 1048576 | tf_op jit(solution)/shard_map/all_to_all | solution.py:44
  82.5 4.3 %all-to-all-start.2 = ((f32[4,1,8,4096]{3,2,1,0:T(8,128)}), f32[4,1,8,4096]{3,2,1,0:T(8,128)}, u32[]{:S(2)}, u32[]{:S(2)}) async-start(f32[4,1,8,4096]{3,2,1,0:T(8,128)} %get-tuple-element.50), calls=%async_computation.2 | async-start | bytes 1048576 | tf_op jit(solution)/shard_map/all_to_all | solution.py:44
  86.8 6.8 %all-to-all-done.2 = f32[4,1,8,4096]{3,2,1,0:T(8,128)} async-done(((f32[4,1,8,4096]{3,2,1,0:T(8,128)}), f32[4,1,8,4096]{3,2,1,0:T(8,128)}, u32[]{:S(2)}, u32[]{:S(2)}) %all-to-all-start.2) | async-done | bytes 524320 | tf_op jit(solution)/shard_map/all_to_all | solution.py:44
  93.6 1.4 fusion.66
  95.4 1.1 broadcast.302
  96.5 10.8 %while.3 = (s32[]{:T(128)}, f32[4,16,6176]{2,1,0:T(8,128)S(1)}, s32[4,3]{1,0:T(4,128)S(1)}, f32[4,16,4096]{2,1,0:T(8,128)}, s32[]{:T(128)}) while((s32[]{:T(128)}, f32[4,16,6176]{2,1,0:T(8,128)S(1)}, s32[4,3]{1,0:T(4,128)S(1)}, f32[4,16,4096]{2,1,0:T(8,128)}, s32[]{:T(128)}) %tuple.61), condition=%wide.while_cond.1, body=%wide.while_body.1.sunk | while | flops 2 | bytes 525929 | solution.py:64
  96.5 0.6 fusion.104
  97.1 2.1 %dynamic-slice_dynamic-update-slice_fusion.5 = f32[4,16,4096]{2,1,0:T(8,128)} fusion(f32[4,16,4096]{2,1,0:T(8,128)} %get-tuple-element.170, s32[]{:T(128)} %get-tuple-element.167, f32[4,16,6176]{2,1,0:T(8,128)S(1)} %get-tuple-element.173, s32[]{:T(128)} %bitcast.43, s32[]{:T(128)} %bitcast.44), kind=kLoop, calls=%fused_computation.6.clone.1 | loop fusion | bytes 525824 | tf_op jit(solution)/shard_map/vmap()/gather
  99.2 0.6 fusion.104
  99.7 2.1 %dynamic-slice_dynamic-update-slice_fusion.5 = f32[4,16,4096]{2,1,0:T(8,128)} fusion(f32[4,16,4096]{2,1,0:T(8,128)} %get-tuple-element.170, s32[]{:T(128)} %get-tuple-element.167, f32[4,16,6176]{2,1,0:T(8,128)S(1)} %get-tuple-element.173, s32[]{:T(128)} %bitcast.43, s32[]{:T(128)} %bitcast.44), kind=kLoop, calls=%fused_computation.6.clone.1 | loop fusion | bytes 525824 | tf_op jit(solution)/shard_map/vmap()/gather
  101.9 0.6 fusion.104
  102.4 2.1 %dynamic-slice_dynamic-update-slice_fusion.5 = f32[4,16,4096]{2,1,0:T(8,128)} fusion(f32[4,16,4096]{2,1,0:T(8,128)} %get-tuple-element.170, s32[]{:T(128)} %get-tuple-element.167, f32[4,16,6176]{2,1,0:T(8,128)S(1)} %get-tuple-element.173, s32[]{:T(128)} %bitcast.43, s32[]{:T(128)} %bitcast.44), kind=kLoop, calls=%fused_computation.6.clone.1 | loop fusion | bytes 525824 | tf_op jit(solution)/shard_map/vmap()/gather
  104.6 0.6 fusion.104
  105.2 2.1 %dynamic-slice_dynamic-update-slice_fusion.5 = f32[4,16,4096]{2,1,0:T(8,128)} fusion(f32[4,16,4096]{2,1,0:T(8,128)} %get-tuple-element.170, s32[]{:T(128)} %get-tuple-element.167, f32[4,16,6176]{2,1,0:T(8,128)S(1)} %get-tuple-element.173, s32[]{:T(128)} %bitcast.43, s32[]{:T(128)} %bitcast.44), kind=kLoop, calls=%fused_computation.6.clone.1 | loop fusion | bytes 525824 | tf_op jit(solution)/shard_map/vmap()/gather
  107.3 1.3 broadcast_select_fusion
  108.6 1.9 %fusion.64 = f32[6,16,4096]{2,0,1:T(8,128)S(1)} fusion(f32[4,16,4096]{2,1,0:T(8,128)S(1)} %get-tuple-element.48, s32[4]{0:T(128)S(1)} %and_select_fusion), kind=kOutput, calls=%fused_computation.91 | convolution fusion | flops 18874392 | bytes 2621456 | tf_op jit(solution)/shard_map/op,pxf->oxf/dot_general | solution.py:119
  110.5 2.1 %convolution_add_fusion = f32[6,16,4096]{2,0,1:T(8,128)S(1)} fusion(f32[6,16,4096]{2,0,1:T(8,128)S(1)} %fusion.64, f32[4,16,4096]{2,1,0:T(8,128)S(1)} %broadcast_select_fusion, s32[4]{0:T(128)S(1)} %get-tuple-element.40), kind=kOutput, calls=%fused_computation.8 | convolution fusion | flops 19267608 | bytes 4194320 | tf_op jit(solution)/shard_map/op,pxf->oxf/dot_general | solution.py:120
  112.6 0.6 fusion.85
  113.2 9.5 %collective-permute-start.4 = (f32[2,16,4096]{2,0,1:T(2,128)S(1)}, f32[2,16,4096]{2,0,1:T(2,128)S(1)}, u32[]{:S(2)}, u32[]{:S(2)}) collective-permute-start(f32[2,16,4096]{2,0,1:T(2,128)S(1)} %get-tuple-element.45), channel_id=1, source_target_pairs={{0,4},{4,8},{8,12},{12,16},{16,20},{20,24},{24,28},{28,32},{32,36}... | collective-permute-start | bytes 1572872 | tf_op jit(solution)/shard_map/ppermute | solution.py:16
  122.7 1.9 %collective-permute-start.5 = (f32[2,16,4096]{2,0,1:T(2,128)S(1)}, f32[2,16,4096]{2,0,1:T(2,128)S(1)}, u32[]{:S(2)}, u32[]{:S(2)}) collective-permute-start(f32[2,16,4096]{2,0,1:T(2,128)S(1)} %get-tuple-element.46), channel_id=1, source_target_pairs={{0,8},{4,12},{8,16},{12,20},{16,24},{20,28},{24,32},{28,36},{32,40... | collective-permute-start | bytes 1572872 | tf_op jit(solution)/shard_map/ppermute | solution.py:16
  124.6 7.3 %collective-permute-done.4 = f32[2,16,4096]{2,0,1:T(2,128)S(1)} collective-permute-done((f32[2,16,4096]{2,0,1:T(2,128)S(1)}, f32[2,16,4096]{2,0,1:T(2,128)S(1)}, u32[]{:S(2)}, u32[]{:S(2)}) %collective-permute-start.4) | collective-permute-done | bytes 524320 | tf_op jit(solution)/shard_map/ppermute | solution.py:16
  131.9 13.0 %collective-permute-done.5 = f32[2,16,4096]{2,0,1:T(2,128)S(1)} collective-permute-done((f32[2,16,4096]{2,0,1:T(2,128)S(1)}, f32[2,16,4096]{2,0,1:T(2,128)S(1)}, u32[]{:S(2)}, u32[]{:S(2)}) %collective-permute-start.5) | collective-permute-done | bytes 524320 | tf_op jit(solution)/shard_map/ppermute | solution.py:16
  144.9 0.5 fusion.67
  145.3 1.1 copy.15
  (45 shorter events, 4.1 us)
Async XLA Ops:
  0.0 26.8 %copy-start = (f32[2,16,4096]{2,1,0:T(8,128)S(1)}, f32[2,16,4096]{2,1,0:T(8,128)}, u32[]{:S(2)}) copy-start(f32[2,16,4096]{2,1,0:T(8,128)} %param.4) | copy-start | bytes 1572868
  0.0 16.6 %copy-start.2 = (s32[4]{0:T(128)S(1)}, s32[4]{0:T(128)}, u32[]{:S(2)}) copy-start(s32[4]{0:T(128)} %param.6) | copy-start | bytes 52
  0.0 16.7 %copy-start.3 = (s32[4]{0:T(128)S(1)}, s32[4]{0:T(128)}, u32[]{:S(2)}) copy-start(s32[4]{0:T(128)} %param.7) | copy-start | bytes 52
  0.8 15.9 %collective-permute-start = (f32[2,2]{0,1:T(2,128)S(1)}, f32[2,2]{0,1:T(2,128)S(1)}, u32[]{:S(2)}, u32[]{:S(2)}) collective-permute-start(f32[2,2]{0,1:T(2,128)S(1)} %convert_element_type.54), channel_id=1, source_target_pairs={{4,0},{8,4},{12,8},{16,12},{20,16},{24,20},{28,24},{32,28},{36,32}... | collective-permute-start | bytes 56 | tf_op jit(solution)/shard_map/ppermute | solution.py:16
  3.4 13.3 %collective-permute-start.1 = (f32[2,2]{0,1:T(2,128)S(1)}, f32[2,2]{0,1:T(2,128)S(1)}, u32[]{:S(2)}, u32[]{:S(2)}) collective-permute-start(f32[2,2]{0,1:T(2,128)S(1)} %convert_element_type.54), channel_id=1, source_target_pairs={{8,0},{12,4},{16,8},{20,12},{24,16},{28,20},{32,24},{36,28},{40,32... | collective-permute-start | bytes 56 | tf_op jit(solution)/shard_map/ppermute | solution.py:16
  7.6 13.9 %collective-permute-start.2 = (f32[2,16,4096]{2,1,0:T(8,128)}, f32[2,16,4096]{2,1,0:T(8,128)S(1)}, u32[]{:S(2)}, u32[]{:S(2)}) collective-permute-start(f32[2,16,4096]{2,1,0:T(8,128)} %param.4), channel_id=1, source_target_pairs={{4,0},{8,4},{12,8},{16,12},{20,16},{24,20},{28,24},{32,28},{36,32}... | collective-permute-start | bytes 1572872 | tf_op jit(solution)/shard_map/ppermute | solution.py:16
  10.6 16.2 %collective-permute-start.3 = (f32[2,16,4096]{2,1,0:T(8,128)}, f32[2,16,4096]{2,1,0:T(8,128)}, u32[]{:S(2)}, u32[]{:S(2)}) collective-permute-start(f32[2,16,4096]{2,1,0:T(8,128)} %param.4), channel_id=1, source_target_pairs={{8,0},{12,4},{16,8},{20,12},{24,16},{28,20},{32,24},{36,28},{40,32... | collective-permute-start | bytes 1572872 | tf_op jit(solution)/shard_map/ppermute | solution.py:16
  21.5 0.8 copy-start.1
  45.6 15.0 %all-to-all-start = ((f32[4,16,4096]{2,1,0:T(8,128)}), f32[4,16,4096]{2,1,0:T(8,128)S(1)}, u32[]{:S(2)}, u32[]{:S(2)}) async-start(f32[4,16,4096]{2,1,0:T(8,128)} %multiply_multiply_fusion), calls=%async_computation | async-start | bytes 2097152 | tf_op jit(solution)/shard_map/all_to_all | solution.py:112
  82.5 11.1 %all-to-all-start.2 = ((f32[4,1,8,4096]{3,2,1,0:T(8,128)}), f32[4,1,8,4096]{3,2,1,0:T(8,128)}, u32[]{:S(2)}, u32[]{:S(2)}) async-start(f32[4,1,8,4096]{3,2,1,0:T(8,128)} %get-tuple-element.50), calls=%async_computation.2 | async-start | bytes 1048576 | tf_op jit(solution)/shard_map/all_to_all | solution.py:44
  113.2 18.7 %collective-permute-start.4 = (f32[2,16,4096]{2,0,1:T(2,128)S(1)}, f32[2,16,4096]{2,0,1:T(2,128)S(1)}, u32[]{:S(2)}, u32[]{:S(2)}) collective-permute-start(f32[2,16,4096]{2,0,1:T(2,128)S(1)} %get-tuple-element.45), channel_id=1, source_target_pairs={{0,4},{4,8},{8,12},{12,16},{16,20},{20,24},{24,28},{28,32},{32,36}... | collective-permute-start | bytes 1572872 | tf_op jit(solution)/shard_map/ppermute | solution.py:16
  122.7 22.2 %collective-permute-start.5 = (f32[2,16,4096]{2,0,1:T(2,128)S(1)}, f32[2,16,4096]{2,0,1:T(2,128)S(1)}, u32[]{:S(2)}, u32[]{:S(2)}) collective-permute-start(f32[2,16,4096]{2,0,1:T(2,128)S(1)} %get-tuple-element.46), channel_id=1, source_target_pairs={{0,8},{4,12},{8,16},{12,20},{16,24},{20,28},{24,32},{28,36},{32,40... | collective-permute-start | bytes 1572872 | tf_op jit(solution)/shard_map/ppermute | solution.py:16
where the time goes:
time: 147 us; the launch traced here: 146 us
  waiting for transfers between devices  46.1 us (31%)
  local copies, waits for them, and re-layouts  41 us (28%)
  starting transfers between devices  32.5 us (22%)
  other arithmetic  12.4 us (8%)
  blocking collectives  10 us (7%)
  matrix products  3.95 us (3%)
    ppermute x6, waiting for transfers between devices, passed_along(): return lax.ppermute(x, axis, pairs)  28.3 us
    ppermute x6, starting transfers between devices, passed_along(): return lax.ppermute(x, axis, pairs)  24.2 us
    gather x24, local copies, waits for them, and re-layouts  22.5 us
    all_to_all x1, waiting for transfers between devices, per_device(): lax.all_to_all(density, 'quad', split_axis=0, concat_axis=1, tiled=True)  11 us
    all_to_all x1, blocking collectives, exchange_in_pieces(): lax.all_to_all(slab, axis, split_axis=0, concat_axis=0, tiled=True)  10 us
    all_to_all x1, waiting for transfers between devices, exchange_in_pieces(): lax.all_to_all(slab, axis, split_axis=0, concat_axis=0, tiled=True)  6.8 us
    add x7, other arithmetic, solve_boxes(): potential = potential + weights[k] * (density - applied) / 6.5  5.95 us
    all_to_all x1, starting transfers between devices, exchange_in_pieces(): lax.all_to_all(slab, axis, split_axis=0, concat_axis=0, tiled=True)  4.32 us
  transfers between devices with their start and end apart: 8, of which 6 were waited for; matrix products, arithmetic and copies ran while one was open for 3% of the time, Pallas kernels for 0%

commit v1 on v0

v1 whole, which is shorter than its diff:
```python
import functools
import math

import jax
import jax.numpy as jnp
import numpy as np
from jax import lax
from jax.experimental import pallas as pl
from jax.experimental.pallas import tpu as pltpu
from jax.sharding import PartitionSpec as P

BZ = 64
SWEEPS = 8
LANES = 128
ROWS = 16
CHUNKS = 32
HALO = SWEEPS - 1
PAD = 10
SHELL = 8


def passed_along(x, axis, by):
    size = lax.axis_size(axis)
    pairs = [(i, i + by) for i in range(size) if 0 <= i + by < size]
    return lax.ppermute(x, axis, pairs)


def even_coefficients():
    nodes = np.polynomial.chebyshev.Chebyshev.basis(SWEEPS).convert(kind=np.polynomial.Polynomial)
    top = nodes.coef / 6.0 ** np.arange(SWEEPS + 1)
    rest = -top / float(nodes(6.5 / 6.0))
    rest[0] += 1.0
    even = rest[::2]
    g = np.zeros(SWEEPS // 2)
    carry = 0.0
    for k in range(SWEEPS // 2):
        g[k] = (even[k] + carry) / 42.25
        carry = g[k]
    return g


def slot_scalars(slot, right_ref, live_ref, c0_ref, c1_ref, c2_ref):
    right = right_ref[slot]
    row = right % 2
    step = right // 2
    left = slot % 2

    def corner(dim):
        near = c0_ref[row, dim].astype(jnp.float32)
        far = jnp.where(step == 1, c1_ref[row, dim], c2_ref[row, dim])
        return jnp.where(step == 0, near, far).astype(jnp.int32) - c0_ref[left, dim]

    return left, right, row, step, live_ref[slot], corner(0), corner(1)


def shift_parts(shift_y, shift_z):
    shift = shift_y * BZ + shift_z
    whole = shift >> 7
    part = shift & (LANES - 1)
    lane = lax.broadcasted_iota(jnp.int32, (ROWS, LANES), 1)
    source = (lane & (BZ - 1)) - shift_z
    keep = (source >= 0) & (source < BZ)
    return whole, part, keep & (lane >= part), keep & (lane < part)


def lanes_of(t):
    return pl.ds(t * LANES, LANES)


def density_kernel(right_ref, live_ref, c0_ref, c1_ref, c2_ref, own_ref, near_ref, far_ref,
                   moved_ref, up_ref, down_ref, rolled):
    rolled[...] = jnp.zeros_like(rolled)

    def one_slot(slot, _):
        left, right, row, step, live, dy, dz = slot_scalars(
            slot, right_ref, live_ref, c0_ref, c1_ref, c2_ref)
        whole, part, first, second = shift_parts(dy, dz)
        for k, source in enumerate((own_ref, near_ref, far_ref)):
            @pl.when(step == k)
            def _():
                for t in range(CHUNKS):
                    rolled[PAD + t] = pltpu.roll(source[row, :, lanes_of(t)], part, 1)
        scale = live.astype(jnp.float32)
        for t in range(CHUNKS):
            at = PAD + t - whole
            moved = jnp.where(first, rolled[at], jnp.where(second, rolled[at - 1], 0.0))
            moved_ref[slot, t] = moved
            density = own_ref[left, :, lanes_of(t)] * moved * scale
            up_ref[slot, HALO * t : HALO * (t + 1), :] = density[ROWS - HALO :]
            down_ref[slot, HALO * t : HALO * (t + 1), :] = density[:HALO]
        return 0

    lax.fori_loop(0, right_ref.shape[0], one_slot, 0)


def solve_kernel(coef, right_ref, live_ref, edge_ref, c0_ref, c1_ref, c2_ref, own_ref, moved_ref,
                 low_ref, high_ref, self_ref, near_ref, far_ref, dens, ping, pong, rolled):
    full = 4 * SHELL
    lane = lax.broadcasted_iota(jnp.int32, (full, LANES), 1)
    at_row = lax.broadcasted_iota(jnp.int32, (full, LANES), 0)
    lower_half = lane < BZ
    zpos = lane & (BZ - 1)
    has_lower = zpos > 0
    has_upper = zpos < BZ - 1
    keep_low = edge_ref[0]
    keep_high = edge_ref[1]
    inside = jnp.where(at_row < SHELL, keep_low, jnp.where(at_row >= 3 * SHELL, keep_high, 1.0))

    for field in (dens, ping, pong, rolled):
        field[...] = jnp.zeros_like(field)
    for out in (self_ref, near_ref, far_ref):
        out[...] = jnp.zeros_like(out)

    def neighbours(field, t, lo, hi):
        n = hi - lo
        here = field[t + 1, lo:hi, :]
        turned = [pltpu.roll(field[t + 1 + d, lo:hi, :], BZ, 1) for d in (-1, 0, 1)]
        total = field[t + 1, lo - 1 : hi - 1, :] + field[t + 1, lo + 1 : hi + 1, :]
        total = total + (turned[1] + jnp.where(lower_half[:n], turned[0], turned[2]))
        below = jnp.where(has_lower[:n], pltpu.roll(here, 1, 1), 0.0)
        above = jnp.where(has_upper[:n], pltpu.roll(here, LANES - 1, 1), 0.0)
        return here, total + (below + above)

    lo, hi = SHELL, SHELL + full

    def sweep(source, target, weight):
        for t in range(CHUNKS):
            _, total = neighbours(source, t, lo, hi)
            if weight is not None:
                total = total + weight * dens[t + 1, lo:hi, :]
            target[t + 1, lo:hi, :] = total * inside

    def one_slot(slot, _):
        left, right, row, step, live, dy, dz = slot_scalars(
            slot, right_ref, live_ref, c0_ref, c1_ref, c2_ref)
        scale = live.astype(jnp.float32)
        for t in range(CHUNKS):
            dens[t + 1, 2 * SHELL : 4 * SHELL, :] = (
                own_ref[left, :, lanes_of(t)] * moved_ref[slot, t] * scale)
            dens[t + 1, 2 * SHELL - HALO : 2 * SHELL, :] = low_ref[slot, HALO * t : HALO * (t + 1), :]
            dens[t + 1, 4 * SHELL : 4 * SHELL + HALO, :] = high_ref[slot, HALO * t : HALO * (t + 1), :]
        sweep(dens, ping, None)
        sweep(ping, pong, coef[2] / coef[3])
        sweep(pong, ping, None)
        sweep(ping, pong, coef[1] / coef[3])
        sweep(pong, ping, None)
        sweep(ping, pong, coef[0] / coef[3])
        whole, part, first, second = shift_parts(-dy, -dz)
        for t in range(CHUNKS):
            here, total = neighbours(pong, t, 2 * SHELL, 4 * SHELL)
            potential = (total + 6.5 * here) * coef[3]
            self_ref[left, :, lanes_of(t)] += potential * moved_ref[slot, t]
            rolled[PAD + t] = pltpu.roll(potential * own_ref[left, :, lanes_of(t)], part, 1)
        for k, target in enumerate((self_ref, near_ref, far_ref)):
            @pl.when(step == k)
            def _():
                for t in range(CHUNKS):
                    at = PAD + t - whole
                    target[row, :, lanes_of(t)] += jnp.where(
                        first, rolled[at], jnp.where(second, rolled[at - 1], 0.0))
        return 0

    lax.fori_loop(0, right_ref.shape[0], one_slot, 0)


def per_device(orbitals, corners, pair_partner, pair_live):
    per_owner, rows, flat = orbitals.shape
    slots = pair_partner.shape[0]
    base = lax.axis_index("wide") * per_owner
    place = lax.axis_index("quad")
    last = lax.axis_size("quad") - 1
    corner_float = corners.astype(jnp.float32)
    near_corner = passed_along(corner_float, "wide", -1)
    far_corner = passed_along(corner_float, "wide", -2)
    near = passed_along(orbitals, "wide", -1)
    far = passed_along(orbitals, "wide", -2)
    right = jnp.clip(pair_partner - base, 0, 3 * per_owner - 1)
    edge = jnp.stack([place > 0, place < last]).astype(jnp.float32)

    smem = pl.BlockSpec(memory_space=pltpu.SMEM)
    vmem = pl.BlockSpec(memory_space=pltpu.VMEM)
    f32 = jnp.float32
    box = jax.ShapeDtypeStruct((per_owner, rows, flat), f32)
    halo = jax.ShapeDtypeStruct((slots, HALO * CHUNKS, LANES), f32)
    moved, up, down = pl.pallas_call(
        density_kernel,
        out_shape=(jax.ShapeDtypeStruct((slots, CHUNKS, ROWS, LANES), f32), halo, halo),
        in_specs=[smem] * 5 + [vmem] * 3,
        out_specs=(vmem,) * 3,
        scratch_shapes=[pltpu.VMEM((CHUNKS + 2 * PAD, ROWS, LANES), f32)],
        cost_estimate=pl.CostEstimate(flops=4_000_000, bytes_accessed=4 << 20, transcendentals=0),
        name="density",
    )(right, pair_live, corners, near_corner, far_corner, orbitals, near, far)
    low = passed_along(up, "quad", 1)
    high = passed_along(down, "quad", -1)
    field = pltpu.VMEM((CHUNKS + 2, 6 * SHELL, LANES), f32)
    mine, to_near, to_far = pl.pallas_call(
        functools.partial(solve_kernel, [float(g) for g in even_coefficients()]),
        out_shape=(box,) * 3,
        in_specs=[smem] * 6 + [vmem] * 4,
        out_specs=(vmem,) * 3,
        scratch_shapes=[field] * 3 + [pltpu.VMEM((CHUNKS + 2 * PAD, ROWS, LANES), f32)],
        cost_estimate=pl.CostEstimate(flops=60_000_000, bytes_accessed=5 << 20, transcendentals=0),
        name="solve",
    )(right, pair_live, edge, corners, near_corner, far_corner, orbitals, moved, low, high)
    from_near = passed_along(to_near, "wide", 1)
    from_far = passed_along(to_far, "wide", 2)
    return mine + from_near + from_far


def solution(mesh):
    in_specs = (P("wide", "quad", None), P("wide", None), P("wide"), P("wide"))
    out_specs = P("wide", "quad", None)
    return jax.shard_map(
        per_device, mesh=mesh, in_specs=in_specs, out_specs=out_specs, check_vma=False
    )
```

time: 147 us -> 102 us (0.69)
  local copies, waits for them, and re-layouts: 41 us -> 3.04 us
  Pallas kernels: 0 us -> 32.5 us
  blocking collectives: 10 us -> 0 us
  waiting for transfers between devices: 46.1 us -> 36.7 us
  other arithmetic: 12.4 us -> 3.75 us
  starting transfers between devices: 32.5 us -> 25.1 us
  matrix products: 3.95 us -> 0 us
    pallas_call x0 -> x2, Pallas kernels: none -> 32.5 us  [the longest x1 29 us: per_device(): pl.pallas_call(functools.partial(solve_kernel, [float(g) for g in even_co...]
    gather x28 -> x0, local copies, waits for them, and re-layouts: 27.6 us -> none
    all_to_all x2 -> x0, waiting for transfers between devices: 17.8 us -> none  [the longest x1 11 us: per_device(): lax.all_to_all(density, 'quad', split_axis=0, concat_axis=1, tiled=True)]
    all_to_all x1 -> x0, blocking collectives: 10 us -> none  [exchange_in_pieces(): lax.all_to_all(slab, axis, split_axis=0, concat_axis=0, tiled=True)]
    ppermute x6 -> x8, waiting for transfers between devices: 28.3 us -> 36.7 us  [passed_along(): return lax.ppermute(x, axis, pairs)]
    all_to_all x2 -> x0, starting transfers between devices: 8.34 us -> none  [the longest x1 4.32 us: exchange_in_pieces(): lax.all_to_all(slab, axis, split_axis=0, concat_axis=0, tiled=True)]
    slice x15 -> x0, local copies, waits for them, and re-layouts: 5.49 us -> none  [the longest x7 2.46 us: neighbours(): total = total + jnp.pad(field[..., BZ:], ((0, 0), (0, 0), (0, BZ)))]
    add x8 -> x1, other arithmetic: 6.41 us -> 1.91 us  [per_device(): return mine + from_near + from_far]
  transfers between devices with their start and end apart: 8 -> 8, of which waited for: 6 -> 6; matrix products, arithmetic and copies ran while one was open for 3% -> 2% of each run, Pallas kernels for 0% -> 0%
where the time goes in v1:
time: 102 us; the launch traced here: 101 us
  waiting for transfers between devices  36.7 us (36%)
  Pallas kernels  32.5 us (32%)
  starting transfers between devices  25.1 us (25%)
  other arithmetic  3.75 us (4%)
  local copies, waits for them, and re-layouts  3.04 us (3%)
    ppermute x8, waiting for transfers between devices, passed_along(): return lax.ppermute(x, axis, pairs)  36.7 us
    pallas_call x1, Pallas kernels, per_device(): pl.pallas_call(functools.partial(solve_kernel, [float(g) for g in even_co...  29 us
    ppermute x8, starting transfers between devices, passed_along(): return lax.ppermute(x, axis, pairs)  25.1 us
    pallas_call x1, Pallas kernels, per_device(): pl.pallas_call(density_kernel, out_shape=(jax.ShapeDtypeStruct((slots, CH...  3.5 us
    unnamed x14, local copies, waits for them, and re-layouts  3.04 us
  transfers between devices with their start and end apart: 8, of which 6 were waited for; matrix products, arithmetic and copies ran while one was open for 2% of the time, Pallas kernels for 0%

profile of v1, /device:TPU:257, one launch (start us, length us, event | category | flops | bytes accessed | tf_op | source)
XLA Modules:
  0.0 101.2 jit_solution(4811447020683028281)
XLA Ops:
  0.0 4.2 %collective-permute-start.3 = (f32[2,16,4096]{2,1,0:T(8,128)}, f32[2,16,4096]{2,1,0:T(8,128)S(1)}, u32[]{:S(2)}, u32[]{:S(2)}) collective-permute-start(f32[2,16,4096]{2,1,0:T(8,128)} %own_ref.3), channel_id=1, source_target_pairs={{8,0},{12,4},{16,8},{20,12},{24,16},{28,20},{32,24},{36,28},{40,32... | collective-permute-start | bytes 1572872 | tf_op jit(solution)/shard_map/ppermute | solution.py:25
  4.2 2.9 %collective-permute-start.2 = (f32[2,16,4096]{2,1,0:T(8,128)}, f32[2,16,4096]{2,1,0:T(8,128)S(1)}, u32[]{:S(2)}, u32[]{:S(2)}) collective-permute-start(f32[2,16,4096]{2,1,0:T(8,128)} %own_ref.3), channel_id=1, source_target_pairs={{4,0},{8,4},{12,8},{16,12},{20,16},{24,20},{28,24},{32,28},{36,32}... | collective-permute-start | bytes 1572872 | tf_op jit(solution)/shard_map/ppermute | solution.py:25
  7.1 0.7 convert_element_type.7
  7.7 3.0 %collective-permute-start.1 = (f32[2,2]{1,0:T(2,128)S(1)}, f32[2,2]{1,0:T(2,128)S(1)}, u32[]{:S(2)}, u32[]{:S(2)}) collective-permute-start(f32[2,2]{1,0:T(2,128)S(1)} %convert_element_type.7), channel_id=1, source_target_pairs={{8,0},{12,4},{16,8},{20,12},{24,16},{28,20},{32,24},{36,28},{40,32... | collective-permute-start | bytes 56 | tf_op jit(solution)/shard_map/ppermute | solution.py:25
  10.7 2.7 %collective-permute-start = (f32[2,2]{1,0:T(2,128)S(1)}, f32[2,2]{1,0:T(2,128)S(1)}, u32[]{:S(2)}, u32[]{:S(2)}) collective-permute-start(f32[2,2]{1,0:T(2,128)S(1)} %convert_element_type.7), channel_id=1, source_target_pairs={{4,0},{8,4},{12,8},{16,12},{20,16},{24,20},{28,24},{32,28},{36,32}... | collective-permute-start | bytes 56 | tf_op jit(solution)/shard_map/ppermute | solution.py:25
  13.4 0.0 copy-start.6
  13.4 0.6 copy-done.6
  14.1 0.5 subtract_clamp_fusion.right_ref
  14.6 0.5 collective-permute-done.1.c2_ref
  15.1 0.0 copy-start.4
  15.1 6.6 %collective-permute-done.c1_ref = f32[2,2]{1,0:T(2,128)S(1)} collective-permute-done((f32[2,2]{1,0:T(2,128)S(1)}, f32[2,2]{1,0:T(2,128)S(1)}, u32[]{:S(2)}, u32[]{:S(2)}) %collective-permute-start) | collective-permute-done | bytes 48 | tf_op jit(solution)/shard_map/ppermute | solution.py:25
  21.7 0.0 copy-start.5
  21.7 0.0 collective-permute-done.3.far_ref
  21.7 0.0 copy-start
  21.7 0.0 collective-permute-done.2.near_ref
  21.7 0.0 copy-done.4
  21.7 0.5 copy-done.5
  22.2 0.3 copy-done
  22.5 0.0 copy-start.1
  22.5 0.8 copy-done.1
  23.3 3.5 %density.1 = (f32[4,32,16,128]{3,2,1,0:T(8,128)}, f32[4,224,128]{2,1,0:T(8,128)}, f32[4,224,128]{2,1,0:T(8,128)}) custom-call(s32[4]{0:T(128)} %subtract_clamp_fusion.right_ref, s32[4]{0:T(128)} %live_ref.3, s32[2,2]{1,0:T(2,128)} %c0_ref.3, f32[2,2]{1,0:T(2,128)} %copy-done.5, f32[2,2]{1,0:T(2,128)} %copy-done.4, f32[2,16,4096]{2,1,0:T(8,128)} %own_ref.3, ...), custom_call_target="tpu_custom_call" | custom-call | flops 4000000 | bytes 4194304 | tf_op jit(solution)/shard_map/density/pallas_call | solution.py:185
  26.8 3.1 %collective-permute-start.4 = (f32[4,224,128]{2,1,0:T(8,128)}, f32[4,224,128]{2,1,0:T(8,128)S(1)}, u32[]{:S(2)}, u32[]{:S(2)}) collective-permute-start(f32[4,224,128]{2,1,0:T(8,128)} %get-tuple-element.12), channel_id=1, source_target_pairs={{0,1},{1,2},{2,3},{4,5},{5,6},{6,7},{8,9},{9,10},{10,11},{12,13},{... | collective-permute-start | bytes 1376264 | tf_op jit(solution)/shard_map/ppermute | solution.py:25
  29.9 1.3 %collective-permute-start.5 = (f32[4,224,128]{2,1,0:T(8,128)}, f32[4,224,128]{2,1,0:T(8,128)S(1)}, u32[]{:S(2)}, u32[]{:S(2)}) collective-permute-start(f32[4,224,128]{2,1,0:T(8,128)} %get-tuple-element.13), channel_id=1, source_target_pairs={{1,0},{2,1},{3,2},{5,4},{6,5},{7,6},{9,8},{10,9},{11,10},{13,12},{... | collective-permute-start | bytes 1376264 | tf_op jit(solution)/shard_map/ppermute | solution.py:25
  31.2 0.7 add_convert_fusion.edge_ref
  31.9 7.6 %collective-permute-done.4.low_ref = f32[4,224,128]{2,1,0:T(8,128)S(1)} collective-permute-done((f32[4,224,128]{2,1,0:T(8,128)}, f32[4,224,128]{2,1,0:T(8,128)S(1)}, u32[]{:S(2)}, u32[]{:S(2)}) %collective-permute-start.4) | collective-permute-done | bytes 458784 | tf_op jit(solution)/shard_map/ppermute | solution.py:25
  39.5 0.0 copy-start.2
  39.5 3.8 %collective-permute-done.5.high_ref = f32[4,224,128]{2,1,0:T(8,128)S(1)} collective-permute-done((f32[4,224,128]{2,1,0:T(8,128)}, f32[4,224,128]{2,1,0:T(8,128)S(1)}, u32[]{:S(2)}, u32[]{:S(2)}) %collective-permute-start.5) | collective-permute-done | bytes 458784 | tf_op jit(solution)/shard_map/ppermute | solution.py:25
  43.3 0.0 copy-start.3
  43.3 0.0 copy-done.2
  43.3 0.8 copy-done.3
  44.0 29.0 %solve.1 = (f32[2,16,4096]{2,1,0:T(8,128)}, f32[2,16,4096]{2,1,0:T(8,128)}, f32[2,16,4096]{2,1,0:T(8,128)}) custom-call(s32[4]{0:T(128)} %subtract_clamp_fusion.right_ref, s32[4]{0:T(128)} %live_ref.3, f32[2]{0:T(128)} %add_convert_fusion.edge_ref, s32[2,2]{1,0:T(2,128)} %c0_ref.3, f32[2,2]{1,0:T(2,128)} %copy-done.5, f32[2,2]{1,0:T(2,128)} %copy-done.4, ...), custom_call_target="tpu_custom_call" | custom-call | flops 60000000 | bytes 5242880 | tf_op jit(solution)/shard_map/solve/pallas_call | solution.py:197
  73.1 4.8 %collective-permute-start.6 = (f32[2,16,4096]{2,1,0:T(8,128)}, f32[2,16,4096]{2,1,0:T(8,128)S(1)}, u32[]{:S(2)}, u32[]{:S(2)}) collective-permute-start(f32[2,16,4096]{2,1,0:T(8,128)} %get-tuple-element.15), channel_id=1, source_target_pairs={{0,4},{4,8},{8,12},{12,16},{16,20},{20,24},{24,28},{28,32},{32,36}... | collective-permute-start | bytes 1572872 | tf_op jit(solution)/shard_map/ppermute | solution.py:25
  77.9 3.2 %collective-permute-start.7 = (f32[2,16,4096]{2,1,0:T(8,128)}, f32[2,16,4096]{2,1,0:T(8,128)S(1)}, u32[]{:S(2)}, u32[]{:S(2)}) collective-permute-start(f32[2,16,4096]{2,1,0:T(8,128)} %get-tuple-element.16), channel_id=1, source_target_pairs={{0,8},{4,12},{8,16},{12,20},{16,24},{20,28},{24,32},{28,36},{32,40... | collective-permute-start | bytes 1572872 | tf_op jit(solution)/shard_map/ppermute | solution.py:25
  81.1 6.3 %collective-permute-done.6 = f32[2,16,4096]{2,1,0:T(8,128)S(1)} collective-permute-done((f32[2,16,4096]{2,1,0:T(8,128)}, f32[2,16,4096]{2,1,0:T(8,128)S(1)}, u32[]{:S(2)}, u32[]{:S(2)}) %collective-permute-start.6) | collective-permute-done | bytes 524320 | tf_op jit(solution)/shard_map/ppermute | solution.py:25
  87.4 11.9 %collective-permute-done.7 = f32[2,16,4096]{2,1,0:T(8,128)S(1)} collective-permute-done((f32[2,16,4096]{2,1,0:T(8,128)}, f32[2,16,4096]{2,1,0:T(8,128)S(1)}, u32[]{:S(2)}, u32[]{:S(2)}) %collective-permute-start.7) | collective-permute-done | bytes 524320 | tf_op jit(solution)/shard_map/ppermute | solution.py:25
  99.3 1.9 %add_add_fusion = f32[2,16,4096]{2,1,0:T(8,128)} fusion(f32[2,16,4096]{2,1,0:T(8,128)S(1)} %collective-permute-done.7, f32[2,16,4096]{2,1,0:T(8,128)} %get-tuple-element.14, f32[2,16,4096]{2,1,0:T(8,128)S(1)} %collective-permute-done.6), kind=kLoop, calls=%fused_computation | loop fusion | flops 262144 | bytes 2097152 | tf_op jit(solution)/shard_map/add | solution.py:208
Async XLA Ops:
  0.0 21.7 %collective-permute-start.3 = (f32[2,16,4096]{2,1,0:T(8,128)}, f32[2,16,4096]{2,1,0:T(8,128)S(1)}, u32[]{:S(2)}, u32[]{:S(2)}) collective-permute-start(f32[2,16,4096]{2,1,0:T(8,128)} %own_ref.3), channel_id=1, source_target_pairs={{8,0},{12,4},{16,8},{20,12},{24,16},{28,20},{32,24},{36,28},{40,32... | collective-permute-start | bytes 1572872 | tf_op jit(solution)/shard_map/ppermute | solution.py:25
  4.2 17.5 %collective-permute-start.2 = (f32[2,16,4096]{2,1,0:T(8,128)}, f32[2,16,4096]{2,1,0:T(8,128)S(1)}, u32[]{:S(2)}, u32[]{:S(2)}) collective-permute-start(f32[2,16,4096]{2,1,0:T(8,128)} %own_ref.3), channel_id=1, source_target_pairs={{4,0},{8,4},{12,8},{16,12},{20,16},{24,20},{28,24},{32,28},{36,32}... | collective-permute-start | bytes 1572872 | tf_op jit(solution)/shard_map/ppermute | solution.py:25
  7.7 7.3 %collective-permute-start.1 = (f32[2,2]{1,0:T(2,128)S(1)}, f32[2,2]{1,0:T(2,128)S(1)}, u32[]{:S(2)}, u32[]{:S(2)}) collective-permute-start(f32[2,2]{1,0:T(2,128)S(1)} %convert_element_type.7), channel_id=1, source_target_pairs={{8,0},{12,4},{16,8},{20,12},{24,16},{28,20},{32,24},{36,28},{40,32... | collective-permute-start | bytes 56 | tf_op jit(solution)/shard_map/ppermute | solution.py:25
  10.7 11.0 %collective-permute-start = (f32[2,2]{1,0:T(2,128)S(1)}, f32[2,2]{1,0:T(2,128)S(1)}, u32[]{:S(2)}, u32[]{:S(2)}) collective-permute-start(f32[2,2]{1,0:T(2,128)S(1)} %convert_element_type.7), channel_id=1, source_target_pairs={{4,0},{8,4},{12,8},{16,12},{20,16},{24,20},{28,24},{32,28},{36,32}... | collective-permute-start | bytes 56 | tf_op jit(solution)/shard_map/ppermute | solution.py:25
  13.4 0.7 copy-start.6
  15.1 6.6 %copy-start.4 = (f32[2,2]{1,0:T(2,128)}, f32[2,2]{1,0:T(2,128)S(1)}, u32[]{:S(2)}) copy-start(f32[2,2]{1,0:T(2,128)S(1)} %collective-permute-done.1.c2_ref) | copy-start | bytes 52
  21.7 0.5 copy-start.5
  21.7 0.8 copy-start
  22.5 0.8 copy-start.1
  26.8 12.7 %collective-permute-start.4 = (f32[4,224,128]{2,1,0:T(8,128)}, f32[4,224,128]{2,1,0:T(8,128)S(1)}, u32[]{:S(2)}, u32[]{:S(2)}) collective-permute-start(f32[4,224,128]{2,1,0:T(8,128)} %get-tuple-element.12), channel_id=1, source_target_pairs={{0,1},{1,2},{2,3},{4,5},{5,6},{6,7},{8,9},{9,10},{10,11},{12,13},{... | collective-permute-start | bytes 1376264 | tf_op jit(solution)/shard_map/ppermute | solution.py:25
  29.9 13.3 %collective-permute-start.5 = (f32[4,224,128]{2,1,0:T(8,128)}, f32[4,224,128]{2,1,0:T(8,128)S(1)}, u32[]{:S(2)}, u32[]{:S(2)}) collective-permute-start(f32[4,224,128]{2,1,0:T(8,128)} %get-tuple-element.13), channel_id=1, source_target_pairs={{1,0},{2,1},{3,2},{5,4},{6,5},{7,6},{9,8},{10,9},{11,10},{13,12},{... | collective-permute-start | bytes 1376264 | tf_op jit(solution)/shard_map/ppermute | solution.py:25
  39.5 3.8 %copy-start.2 = (f32[4,224,128]{2,1,0:T(8,128)}, f32[4,224,128]{2,1,0:T(8,128)S(1)}, u32[]{:S(2)}) copy-start(f32[4,224,128]{2,1,0:T(8,128)S(1)} %collective-permute-done.4.low_ref) | copy-start | bytes 1376260
  43.3 0.8 copy-start.3
  73.1 14.3 %collective-permute-start.6 = (f32[2,16,4096]{2,1,0:T(8,128)}, f32[2,16,4096]{2,1,0:T(8,128)S(1)}, u32[]{:S(2)}, u32[]{:S(2)}) collective-permute-start(f32[2,16,4096]{2,1,0:T(8,128)} %get-tuple-element.15), channel_id=1, source_target_pairs={{0,4},{4,8},{8,12},{12,16},{16,20},{20,24},{24,28},{28,32},{32,36}... | collective-permute-start | bytes 1572872 | tf_op jit(solution)/shard_map/ppermute | solution.py:25
  77.9 21.5 %collective-permute-start.7 = (f32[2,16,4096]{2,1,0:T(8,128)}, f32[2,16,4096]{2,1,0:T(8,128)S(1)}, u32[]{:S(2)}, u32[]{:S(2)}) collective-permute-start(f32[2,16,4096]{2,1,0:T(8,128)} %get-tuple-element.16), channel_id=1, source_target_pairs={{0,8},{4,12},{8,16},{12,20},{16,24},{20,28},{24,32},{28,36},{32,40... | collective-permute-start | bytes 1572872 | tf_op jit(solution)/shard_map/ppermute | solution.py:25
